TPU v7x, 256 devices: a whole 4x4x8 slice. The times are simulated.
256 devices in a mesh: ex: 32 (over x, y, core), cls: 8 (over z).
Axes of the slice: x: 4, y: 4, z: 8, core: 2. Of those that a mesh axis runs over, the one named last changes fastest.
Arguments:
- features: bfloat16 [32768, 1664], P('ex'), may hold values from -16 to 16
- labels: int32 [32768], P('ex'), may hold values from 0 to 11263
- weight: bfloat16 [1664, 11264], P(None, 'cls'), may hold values from -1 to 1
- noise: bfloat16 [1664, 11264], P('ex', 'cls'), may hold values from -5 to 5
Outputs:
- new_weight: bfloat16 [1664, 11264], P(None, 'cls')
All inputs are finite; a program needn't handle non-finite values.
Results may differ from a plain program's by a relative error of at most 0.0013.
Values may be sent and summed in bfloat16 or wider, within the bound.
A program may use at most 128 MiB of HBM per device.

v0:
```python
import jax
import jax.numpy as jnp
from jax import lax
from jax.sharding import PartitionSpec as P


def copy_for_each(shard, axis):
    copies = jnp.broadcast_to(shard, (lax.axis_size(axis), *shard.shape))
    return lax.all_to_all(copies, axis, split_axis=0, concat_axis=0, tiled=True)


def over_copies(shard, axis):
    return copy_for_each(shard, axis).max(axis=0)


def taken_together(shard, axis):
    return copy_for_each(shard, axis).sum(axis=0)


def in_one(arrays, axis):
    ends = [0]
    for a in arrays:
        ends.append(ends[-1] + a.size)
    total = taken_together(jnp.concatenate([a.ravel() for a in arrays]), axis)
    return tuple((total[b:e].reshape(a.shape) for a, b, e in zip(arrays, ends, ends[1:])))


def local(features, labels, weight, noise):
    clip_norm = 48.0
    cls_width = weight.shape[1]
    logits = jnp.dot(features, weight, preferred_element_type=jnp.float32)
    offset = lax.axis_index("cls") * cls_width
    local_lab = labels - offset
    columns = lax.broadcasted_iota(jnp.int32, (1, cls_width), 1)
    onehot = columns == local_lab[:, None]
    label_part = jnp.sum(jnp.where(onehot, logits, 0.0), axis=1)
    top = over_copies(jnp.max(logits, axis=1), "cls")
    expo = jnp.exp(logits - top[:, None])
    total, squares, label_logit = in_one(
        (jnp.sum(expo, axis=1), jnp.sum(expo * expo, axis=1), label_part), "cls"
    )
    probs = expo / total[:, None]
    label_prob = jnp.exp(label_logit - top) / total
    resid_sq = squares / (total * total) - 2.0 * label_prob + 1.0
    resid_norm = jnp.sqrt(jnp.maximum(resid_sq, 0.0))
    feat = features.astype(jnp.float32)
    feat_norm = jnp.sqrt(jnp.sum(feat * feat, axis=1))
    factor = clip_norm / jnp.maximum(feat_norm * resid_norm, clip_norm)
    resid = probs - onehot.astype(jnp.float32)
    coef = (factor[:, None] * resid).astype(jnp.bfloat16)
    partial_grad = lax.dot_general(
        features, coef, (((0,), (0,)), ((), ())), preferred_element_type=jnp.float32
    )
    classes = cls_width * lax.axis_size("cls")
    batch = features.shape[0] * lax.axis_size("ex")
    scale = 0.1 * classes / batch
    grad_part = lax.psum_scatter(partial_grad, "ex", scatter_dimension=1, tiled=True)
    noise_part = lax.all_to_all(noise, "ex", split_axis=1, concat_axis=0, tiled=True)
    span = grad_part.shape[1]
    own_weight = lax.dynamic_slice_in_dim(weight, lax.axis_index("ex") * span, span, 1)
    updated = own_weight.astype(jnp.float32) - scale * (
        grad_part + 0.96 * clip_norm * noise_part.astype(jnp.float32)
    )
    return lax.all_gather(updated.astype(jnp.bfloat16), "ex", axis=1, tiled=True)


def solution(mesh):
    in_specs = (P("ex", None), P("ex"), P(None, "cls"), P("ex", "cls"))
    out_specs = P(None, "cls")
    return jax.shard_map(local, mesh=mesh, in_specs=in_specs, out_specs=out_specs, check_vma=False)
```

profile of v0, /device:TPU:1, one launch (start us, length us, event | category | flops | bytes accessed | tf_op | source)
XLA Modules:
  0.0 255.8 jit_solution(9415256647725124209)
XLA Ops:
  6.5 10.5 %fusion.18 = (f32[1024]{0:T(1024)S(1)}, f32[1024,1408]{1,0:T(8,128)}) fusion(bf16[1024,1664]{1,0:T(8,128)(2,1)} %param.4, bf16[1664,1408]{1,0:T(8,128)(2,1)} %param.6), kind=kOutput, calls=%fused_computation.32 | convolution fusion | flops 4799724544 | bytes 13864960 | tf_op jit(solution)/shard_map/dot_general | solution.py:31
  17.1 0.6 broadcast_in_dim.14
  17.7 9.1 %all-to-all-start = ((f32[8,1,1024]{2,1,0:T(1,128)}), f32[8,1,1024]{2,1,0:T(1,128)S(1)}, u32[]{:S(2)}, u32[]{:S(2)}) async-start(f32[8,1,1024]{2,1,0:T(1,128)} %broadcast_in_dim.14), calls=%async_computation | async-start | bytes 65536 | tf_op jit(solution)/shard_map/all_to_all | solution.py:9
  26.9 2.9 %all_to_all.20 = bf16[52,32,44]{2,1,0:T(8,128)(2,1)} reshape(bf16[52,1408]{1,0:T(8,128)(2,1)} %param.7) | data formatting | bytes 292864 | tf_op jit(solution)/shard_map/all_to_all | solution.py:58
  29.7 2.3 copy.22
  32.0 2.2 reshape.21
  34.3 4.0 %fusion.1 = (f32[1024]{0:T(1024)S(1)}, f32[1024]{0:T(1024)S(1)}, f32[1024]{0:T(1024)S(1)}) fusion(f32[1024,1408]{1,0:T(8,128)} %get-tuple-element.11, f32[1024]{0:T(1024)S(1)} %reduce_max.19, s32[1024]{0:T(1024)S(1)} %broadcast_subtract_fusion), kind=kLoop, calls=%fused_computation.7 | loop fusion | flops 10089472 | bytes 5787648 | tf_op jit(solution)/shard_map/reduce_sum | solution.py:40
  38.2 0.7 broadcast_in_dim.16
  38.9 6.6 %all-to-all-start.1 = ((f32[8,1,3072]{2,1,0:T(1,128)}), f32[8,1,3072]{2,1,0:T(1,128)S(1)}, u32[]{:S(2)}, u32[]{:S(2)}) async-start(f32[8,1,3072]{2,1,0:T(1,128)} %broadcast_in_dim.16), calls=%async_computation.1 | async-start | bytes 196608 | tf_op jit(solution)/shard_map/all_to_all | solution.py:9
  45.6 1.3 multiply_reduce_fusion
  46.9 6.2 %all-to-all-done.1 = f32[8,1,3072]{2,1,0:T(1,128)S(1)} async-done(((f32[8,1,3072]{2,1,0:T(1,128)}), f32[8,1,3072]{2,1,0:T(1,128)S(1)}, u32[]{:S(2)}, u32[]{:S(2)}) %all-to-all-start.1) | async-done | bytes 98336 | tf_op jit(solution)/shard_map/all_to_all | solution.py:9
  53.1 0.6 copy-done.1
  53.8 9.7 %all-to-all-start.2 = ((bf16[32,2,1144]{2,1,0:T(2,128)(2,1)}), bf16[32,2,1144]{2,1,0:T(2,128)(2,1)S(1)}, u32[]{:S(2)}, u32[]{:S(2)}) async-start(bf16[32,2,1144]{2,1,0:T(2,128)(2,1)} %reshape.21), calls=%async_computation.2 | async-start | bytes 294912 | tf_op jit(solution)/shard_map/all_to_all | solution.py:58
  63.8 1.6 reduce_sum.49
  65.3 0.7 maximum_divide_fusion
  66.0 12.5 %convolution_bitcast_fusion = f32[1664,1408]{0,1:T(8,128)} fusion(bf16[1024,1664]{1,0:T(8,128)(2,1)S(1)} %copy-done, f32[1024,1408]{1,0:T(8,128)} %get-tuple-element.11, f32[1024]{0:T(1024)S(1)} %get-tuple-element.9, f32[1024]{0:T(1024)S(1)} %get-tuple-element.8, s32[1024]{0:T(1024)} %copy-done.3, f32[1024]{0:T(1024)} %copy-done.2), kind=kOutput, calls=%fused_computation | convolution fusion | flops 4808376320 | bytes 18563072 | tf_op jit(solution)/shard_map/dot_general | solution.py:51
  78.6 88.6 %fusion = f32[1664,48]{0,1:T(8,128)S(1)} fusion(f32[1664,1408]{0,1:T(8,128)} %convolution_bitcast_fusion), kind=kCustom, calls=%all-reduce-scatter | all-reduce-scatter fusion | flops 2555905 | bytes 9692160
  167.2 2.1 collective-permute-start
  169.4 1.3 collective-permute-start.1
  170.7 1.4 constant_dynamic-slice_fusion
  172.0 0.2 copy.27
  172.3 0.7 dynamic-slice.4
  173.7 0.6 reshape.22
  174.3 1.3 collective-permute-start.2
  175.6 0.2 copy.23
  175.9 0.4 mul.63
  176.3 5.8 %collective-permute-done.2 = f32[1664,28]{0,1:T(8,128)S(1)} collective-permute-done((f32[1664,28]{0,1:T(8,128)S(1)}, f32[1664,28]{0,1:T(8,128)S(1)}, u32[]{:S(2)}, u32[]{:S(2)}) %collective-permute-start.2) | collective-permute-done | bytes 186400
  182.1 0.8 concatenate.4
  182.9 0.8 fusion.9
  183.7 50.5 %all-gather.3.cloned.1.call-done = bf16[32,44,1664]{2,1,0:T(8,128)(2,1)} async-done(((bf16[1,44,1664]{2,1,0:T(8,128)(2,1)}), bf16[32,44,1664]{2,1,0:T(8,128)(2,1)}) %all-gather.3.cloned.1.call-update) | async-done | bytes 4685840 | tf_op jit(solution)/shard_map/all_gather | solution.py:64
  234.2 7.2 %reshape.19 = bf16[1408,1664]{1,0:T(8,128)(2,1)} reshape(bf16[32,44,1664]{2,1,0:T(8,128)(2,1)} %all-gather.3.cloned.1.call-done) | data formatting | bytes 9371648
  241.4 7.6 %copy.24 = bf16[1664,1408]{1,0:T(8,128)(2,1)} copy(bf16[1664,1408]{0,1:T(8,128)(2,1)} %bitcast.20) | data formatting | bytes 9371648
  (22 shorter events, 0.4 us)
Async XLA Ops:
  6.5 20.3 %copy-start.4 = (s32[1024]{0:T(1024)S(1)}, s32[1024]{0:T(1024)}, u32[]{:S(2)}) copy-start(s32[1024]{0:T(1024)} %param.5) | copy-start | bytes 12292
  17.1 28.5 %copy-start = (bf16[1024,1664]{1,0:T(8,128)(2,1)S(1)}, bf16[1024,1664]{1,0:T(8,128)(2,1)}, u32[]{:S(2)}) copy-start(bf16[1024,1664]{1,0:T(8,128)(2,1)} %param.4) | copy-start | bytes 10223620
  17.7 16.5 %all-to-all-start = ((f32[8,1,1024]{2,1,0:T(1,128)}), f32[8,1,1024]{2,1,0:T(1,128)S(1)}, u32[]{:S(2)}, u32[]{:S(2)}) async-start(f32[8,1,1024]{2,1,0:T(1,128)} %broadcast_in_dim.14), calls=%async_computation | async-start | bytes 65536 | tf_op jit(solution)/shard_map/all_to_all | solution.py:9
  26.8 12.1 %copy-start.3 = (s32[1024]{0:T(1024)}, s32[1024]{0:T(1024)S(1)}, u32[]{:S(2)}) copy-start(s32[1024]{0:T(1024)S(1)} %broadcast_subtract_fusion) | copy-start | bytes 12292
  34.3 4.7 %copy-start.2 = (f32[1024]{0:T(1024)}, f32[1024]{0:T(1024)S(1)}, u32[]{:S(2)}) copy-start(f32[1024]{0:T(1024)S(1)} %reduce_max.19) | copy-start | bytes 12292
  38.9 14.2 %all-to-all-start.1 = ((f32[8,1,3072]{2,1,0:T(1,128)}), f32[8,1,3072]{2,1,0:T(1,128)S(1)}, u32[]{:S(2)}, u32[]{:S(2)}) async-start(f32[8,1,3072]{2,1,0:T(1,128)} %broadcast_in_dim.16), calls=%async_computation.1 | async-start | bytes 196608 | tf_op jit(solution)/shard_map/all_to_all | solution.py:9
  53.1 0.6 copy-start.1
  53.8 119.9 %all-to-all-start.2 = ((bf16[32,2,1144]{2,1,0:T(2,128)(2,1)}), bf16[32,2,1144]{2,1,0:T(2,128)(2,1)S(1)}, u32[]{:S(2)}, u32[]{:S(2)}) async-start(bf16[32,2,1144]{2,1,0:T(2,128)(2,1)} %reshape.21), calls=%async_computation.2 | async-start | bytes 294912 | tf_op jit(solution)/shard_map/all_to_all | solution.py:58
  63.5 170.7 %all-gather.3.cloned.1.call-start = ((), (), s32[]{:S(2)}) async-start(), calls=%async_computation.3 | async-start | bytes 5271552 | tf_op jit(solution)/shard_map/all_gather | solution.py:64
  78.6 93.7 %copy-start.5 = (u32[256]{0:T(256)S(1)}, u32[256]{0:T(256)}, u32[]{:S(2)}) copy-start(u32[256]{0:T(256)} %constant.33) | copy-start | bytes 3076
  167.2 14.9 %collective-permute-start = (f32[1664,48]{0,1:T(8,128)S(1)}, f32[1664,48]{0,1:T(8,128)S(1)}, u32[]{:S(2)}, u32[]{:S(2)}) collective-permute-start(f32[1664,48]{0,1:T(8,128)S(1)} %fusion), channel_id=1, source_target_pairs={{0,8},{8,16},{16,24},{24,32},{32,40},{40,48},{48,56},{56,64},{64,7... | collective-permute-start | bytes 958472
  169.4 12.7 %collective-permute-start.1 = (f32[1664,48]{0,1:T(8,128)S(1)}, f32[1664,48]{0,1:T(8,128)S(1)}, u32[]{:S(2)}, u32[]{:S(2)}) collective-permute-start(f32[1664,48]{0,1:T(8,128)S(1)} %fusion), channel_id=1, source_target_pairs={{0,16},{8,24},{16,32},{24,40},{32,48},{40,56},{48,64},{56,72},{64,... | collective-permute-start | bytes 958472
  174.3 7.8 %collective-permute-start.2 = (f32[1664,28]{0,1:T(8,128)S(1)}, f32[1664,28]{0,1:T(8,128)S(1)}, u32[]{:S(2)}, u32[]{:S(2)}) collective-permute-start(f32[1664,28]{0,1:T(8,128)S(1)} %slice.15), channel_id=1, source_target_pairs={{0,24},{8,32},{16,40},{24,48},{32,56},{40,64},{48,72},{56,80},{64,... | collective-permute-start | bytes 559112
Sparse Core Ops, SparseCore 0:
  183.8 50.3 all-gather.2
where the time goes:
time: 257 us; the launch traced here: 256 us
  blocking collectives  88.6 us (34%)
  waiting for transfers between devices  62.5 us (24%)
  starting transfers between devices  30.5 us (12%)
  local copies, waits for them, and re-layouts  28.4 us (11%)
  matrix products  23.1 us (9%)
  between operations  14.2 us (6%)
  other arithmetic  8.44 us (3%)
    unnamed x1, blocking collectives  88.6 us
    all_gather x1, waiting for transfers between devices, local(): lax.all_gather(updated.astype(jnp.bfloat16), 'ex', axis=1, tiled=True)  50.5 us
    unnamed x20, local copies, waits for them, and re-layouts  19.9 us
    all_to_all x2, starting transfers between devices, copy_for_each(): return lax.all_to_all(copies, axis, split_axis=0, concat_axis=0, tiled=True)  15.8 us
    dot_general x1, matrix products, local(): lax.dot_general(features, coef, (((0,), (0,)), ((), ())), preferred_eleme...  12.5 us
    dot_general x1, matrix products, local(): logits = jnp.dot(features, weight, preferred_element_type=jnp.float32)  10.5 us
    all_to_all x1, starting transfers between devices, local(): lax.all_to_all(noise, 'ex', split_axis=1, concat_axis=0, tiled=True)  9.75 us
    all_to_all x2, waiting for transfers between devices, copy_for_each(): return lax.all_to_all(copies, axis, split_axis=0, concat_axis=0, tiled=True)  6.25 us
  transfers between devices with their start and end apart: 7, of which 3 were waited for; matrix products, arithmetic and copies ran while one was open for 44% of the time, Pallas kernels for 0%

commit v1 on v0

v1 whole, which is shorter than its diff:
```python
import functools

import jax
import jax.numpy as jnp
from jax import lax
from jax.experimental import pallas as pl
from jax.experimental.pallas import tpu as pltpu
from jax.sharding import PartitionSpec as P

MESH = pl.DeviceIdType.MESH
F32, BF16 = jnp.float32, jnp.bfloat16
CLIP = 48.0
WIDE = 256
LANES = 128
CUT = 48
ROWS = ((0, 48), (48, 56))


def kernel(scale, f_hbm, lab_ref, w_hbm, noise_hbm, out_ref,
           f_v, w_v, ft_v, e_v, coef_v, lab_v, xt_v, st_v, fn_v, psend_v, precv_v,
           g_v, ra_v, hf_v, hs_v, rb_v, base_v, wown_v, nz_v,
           ld_sem, st_s, st_r, nz_s, nz_r, p_s, p_r, a_s, a_r, b_s, b_r,
           g1_s, g1_r, g2_s, g2_r, g3_s, g3_r, d_s, d_r):
    rows, depth = f_hbm.shape
    width = w_hbm.shape[1]
    n_cls = lax.axis_size("cls")
    ex = lax.axis_index("ex")
    z = lax.axis_index("cls")
    c = ex % 2
    x = ex // 8
    y = (ex // 2) % 4
    a = x * (1 - c) + y * c
    b = y * (1 - c) + x * c

    def spot(i, j):
        return i * (4 - 3 * c) + j * (1 + 3 * c)

    def dev(i, j):
        return spot(i, j) * 2 + c

    mine = spot(a, b)
    a_up, a_dn, a_op = (a + 1) % 4, (a + 3) % 4, (a + 2) % 4
    b_up, b_dn, b_op = (b + 1) % 4, (b + 3) % 4, (b + 2) % 4
    to_aup, to_adn = dev(a_up, b), dev(a_dn, b)
    to_bup, to_bdn = dev(a, b_up), dev(a, b_dn)
    partner = ex + 1 - 2 * c

    barrier = pltpu.get_barrier_semaphore()
    for t in (to_aup, to_adn, to_bup, to_bdn, partner):
        pl.semaphore_signal(barrier, inc=1, device_id={"ex": t}, device_id_type=MESH)
    for k in range(1, n_cls):
        pl.semaphore_signal(barrier, inc=1, device_id={"cls": (z + k) % n_cls}, device_id_type=MESH)

    def send(src, dst, s, r, t):
        return pltpu.make_async_remote_copy(
            src_ref=src, dst_ref=dst, send_sem=s, recv_sem=r, device_id={"ex": t}, device_id_type=MESH)

    loads = [
        pltpu.make_async_copy(f_hbm, f_v, ld_sem.at[0]),
        pltpu.make_async_copy(w_hbm, w_v, ld_sem.at[1]),
        pltpu.make_async_copy(w_hbm.at[pl.ds(pl.multiple_of(mine * 104, 8), 104), :], wown_v, ld_sem.at[2]),
        pltpu.make_async_copy(noise_hbm, nz_v.at[c], ld_sem.at[3]),
    ]
    for cp in loads:
        cp.start()

    for i in range(rows // LANES):
        row = jnp.broadcast_to(lab_ref[i:i + 1, :].astype(F32), (LANES, LANES))
        lab_v[i * LANES:(i + 1) * LANES, :] = row.T.astype(jnp.int32) - z * width
    lane = lax.broadcasted_iota(jnp.int32, (64, LANES), 1)

    for cp in loads:
        cp.wait()
    pl.semaphore_wait(barrier, 5 + n_cls - 1)
    nz = send(noise_hbm, nz_v.at[c], nz_s, nz_r, partner)
    nz.start()

    tiles = width // LANES

    def st_copy(blk, k):
        return pltpu.make_async_remote_copy(
            src_ref=st_v.at[z, blk], dst_ref=st_v.at[z, blk], send_sem=st_s.at[blk, k - 1],
            recv_sem=st_r.at[blk, k - 1], device_id={"cls": (z + k) % n_cls}, device_id_type=MESH)

    def forward(blk, _):
        r256 = pl.ds(pl.multiple_of(blk * 256, 256), 256)
        for n in range(0, width, WIDE):
            w = min(WIDE, width - n)
            e_v[r256, n:n + w] = jnp.dot(f_v[r256, :], w_v[:, n:n + w], preferred_element_type=F32)
        for h in range(2):
            r128 = pl.ds(pl.multiple_of(blk * 256 + h * 128, 128), 128)
            ft_v[:, r128] = f_v[r128, :].T
            for s in range(2):
                r = pl.ds(pl.multiple_of(blk * 256 + h * 128 + s * 64, 64), 64)
                top = e_v[r, 0:LANES]
                for n in range(1, tiles):
                    top = jnp.maximum(top, e_v[r, n * LANES:(n + 1) * LANES])
                top = jnp.max(top, axis=1, keepdims=True)
                lab = lab_v[r, :]
                one = jnp.zeros((64, LANES), F32)
                two, hit, sq = one, one, one
                for n in range(tiles):
                    cols = slice(n * LANES, (n + 1) * LANES)
                    v = jnp.exp(e_v[r, cols] - top)
                    e_v[r, cols] = v
                    one += v
                    two += v * v
                    hit += jnp.where(lane + n * LANES == lab, v, 0.0)
                for k in range(depth // LANES):
                    v = f_v[r, k * LANES:(k + 1) * LANES].astype(F32)
                    sq += v * v
                one = jnp.sum(one, axis=1, keepdims=True)
                two = jnp.sum(two, axis=1, keepdims=True)
                hit = jnp.sum(hit, axis=1, keepdims=True)
                sq = jnp.sum(sq, axis=1, keepdims=True)
                pick = jnp.where(lane == 4 * h, top, 0.0)
                pick = jnp.where(lane == 4 * h + 1, one, pick)
                pick = jnp.where(lane == 4 * h + 2, two, pick)
                pick = jnp.where(lane == 4 * h + 3, hit, pick)
                pick = jnp.where(lane == 8 + h, sq, pick)
                if h == 0:
                    xt_v[s * 64:(s + 1) * 64, :] = pick
                else:
                    xt_v[s * 64:(s + 1) * 64, :] += pick
        t = xt_v[...].T
        st_v[z, blk] = t[0:8]
        fn_v[blk] = t[8:16]
        for k in range(1, n_cls):
            st_copy(blk, k).start()
        return 0

    lax.fori_loop(0, rows // 256, forward, 0)

    nz.wait_recv()
    for n in range(0, width, WIDE):
        w = min(WIDE, width - n)
        base_v[n // WIDE, :, 0:w] = wown_v[:, n:n + w].astype(F32)
        for i in range(2):
            base_v[n // WIDE, i * 52:(i + 1) * 52, 0:w] -= (scale * 0.96 * CLIP) * nz_v[i, :, n:n + w].astype(F32)

    def weigh(blk, _):
        for k in range(1, n_cls):
            st_copy(blk, k).wait_recv()
        for h in range(2):
            tops = [st_v[p, blk, 4 * h:4 * h + 1, :] for p in range(n_cls)]
            top = functools.reduce(jnp.maximum, tops)
            total = jnp.zeros((1, LANES), F32)
            squares, hit = total, total
            for p in range(n_cls):
                g = jnp.exp(tops[p] - top)
                total += st_v[p, blk, 4 * h + 1:4 * h + 2, :] * g
                squares += st_v[p, blk, 4 * h + 2:4 * h + 3, :] * (g * g)
                hit += st_v[p, blk, 4 * h + 3:4 * h + 4, :] * g
            prob = hit / total
            miss = 1.0 - prob
            resid = jnp.maximum(squares / (total * total) - prob * prob, 0.0) + miss * miss
            norm = jnp.sqrt(fn_v[blk, h:h + 1, :]) * jnp.sqrt(resid)
            factor = CLIP / jnp.maximum(norm, CLIP)
            up = factor * jnp.exp(st_v[z, blk, 4 * h:4 * h + 1, :] - top) / total
            up = jnp.broadcast_to(up, (LANES, LANES)).T
            down = jnp.broadcast_to(factor, (LANES, LANES)).T
            for s in range(2):
                r = pl.ds(pl.multiple_of(blk * 256 + h * 128 + s * 64, 64), 64)
                lab = lab_v[r, :]
                u, d = up[s * 64:(s + 1) * 64], down[s * 64:(s + 1) * 64]
                for n in range(tiles):
                    v = e_v[r, n * LANES:(n + 1) * LANES] * u
                    v -= jnp.where(lane + n * LANES == lab, d, 0.0)
                    coef_v[n // 2, r, (n % 2) * LANES:(n % 2 + 1) * LANES] = v.astype(BF16)
        return 0

    lax.fori_loop(0, rows // 256, weigh, 0)

    def tile_of(t):
        return pl.ds(pl.multiple_of(t * 416, 32), 416)

    def p_send(j, w):
        return send(psend_v.at[j, :, pl.ds(0, w)], precv_v.at[j, :, pl.ds(0, w)], p_s.at[j], p_r.at[j], partner)

    def part(j, w, wp):
        def body(t, _):
            psend_v[j, tile_of(t), 0:wp] = jnp.dot(
                ft_v[tile_of(t), :], coef_v[(1 - c) * 3 + j, :, 0:wp], preferred_element_type=F32)
            return 0
        lax.fori_loop(0, 4, body, 0)
        p_send(j, wp).start()

    def a_msg(j, w, k):
        group, half, t = ((a_op, 0, to_aup), (a_op, 1, to_adn), (a_up, 1, to_aup),
                          (a_dn, 0, to_adn), (a_up, 0, to_aup), (a_dn, 1, to_adn))[k]
        return send(g_v.at[j, group, pl.ds(2 * half, 2), :, pl.ds(0, w)], ra_v.at[j, k, :, :, pl.ds(0, w)],
                    a_s.at[j, k], a_r.at[j, k], t)

    def own(j, w, wp):
        p_send(j, w).wait_recv()

        def body(t, _):
            acc = jnp.dot(ft_v[tile_of(t), :], coef_v[c * 3 + j, :, 0:w], preferred_element_type=F32)
            acc += precv_v[j, tile_of(t), 0:w]
            for i in range(4):
                q = spot(t, i)
                g_v[j, q // 4, q % 4, :, 0:w] = acc[i * 104:(i + 1) * 104].astype(BF16)
            return 0
        lax.fori_loop(0, 4, body, 0)
        for k in range(4):
            a_msg(j, w, k).start()

    def r1(j, w, wp):
        for k, group, half in ((0, a_up, 0), (1, a_dn, 1)):
            a_msg(j, w, k).wait_recv()
            for i in range(2):
                v = g_v[j, group, 2 * half + i, :, 0:w].astype(F32) + ra_v[j, k, i, :, 0:w].astype(F32)
                g_v[j, group, 2 * half + i, :, 0:w] = v.astype(BF16)
            a_msg(j, w, 4 + k).start()

    def b_msg(j, w, k):
        piece, half, t = ((b_op, 0, to_bup), (b_op, 1, to_bdn), (b_up, 1, to_bup),
                          (b_dn, 0, to_bdn), (b_up, 0, to_bup), (b_dn, 1, to_bdn))[k]
        r0, nr = ROWS[half]
        return send(hs_v.at[j, piece, pl.ds(r0, nr), pl.ds(0, w)], rb_v.at[j, k, pl.ds(0, nr), pl.ds(0, w)],
                    b_s.at[j, k], b_r.at[j, k], t)

    def r2(j, w, wp):
        for k in (2, 3, 4, 5):
            a_msg(j, w, k).wait_recv()
        for half, dep, ind in ((0, 4, 3), (1, 5, 2)):
            for i in range(2):
                piece = 2 * half + i
                v = g_v[j, a, piece, :, 0:w].astype(F32) + ra_v[j, dep, i, :, 0:w].astype(F32)
                v += ra_v[j, ind, i, :, 0:w].astype(F32)
                hf_v[j, piece, :, 0:w] = v
                hs_v[j, piece, :, 0:w] = v.astype(BF16)
        for k in range(4):
            b_msg(j, w, k).start()

    def r3(j, w, wp):
        for k, piece, half in ((0, b_up, 0), (1, b_dn, 1)):
            r0, nr = ROWS[half]
            b_msg(j, w, k).wait_recv()
            v = hf_v[j, piece, r0:r0 + nr, 0:w] + rb_v[j, k, 0:nr, 0:w].astype(F32)
            hs_v[j, piece, r0:r0 + nr, 0:w] = v.astype(BF16)
            b_msg(j, w, 4 + k).start()

    def cols(j, w, core):
        return pl.ds(pl.multiple_of(core * 3 * WIDE + j * WIDE, LANES), w)

    def place(j, w, p, core, half=None):
        if half is None:
            return out_ref.at[p, :, cols(j, w, core)]
        return out_ref.at[p, pl.ds(*ROWS[half]), cols(j, w, core)]

    def g1(j, w, k):
        piece, half, t = ((mine, None, to_bup), (mine, None, to_bdn),
                          (spot(a, b_dn), 0, to_bup), (spot(a, b_up), 1, to_bdn))[k]
        ref = place(j, w, piece, c, half)
        return send(ref, ref, g1_s.at[j, k], g1_r.at[j, k], t)

    near = (b, b_dn, b_up, b_op)

    def g2(j, w, r, up):
        ref = place(j, w, spot(a, near[r]), c)
        return send(ref, ref, g2_s.at[j, 2 * r + up], g2_r.at[j, 2 * r + up], to_aup if up else to_adn)

    def g3(j, w, r):
        ref = place(j, w, spot(a_dn if r < 2 else a_up, near[r]), c)
        return send(ref, ref, g3_s.at[j, r], g3_r.at[j, r], to_aup if r < 2 else to_adn)

    def d2d(j, w, i, r, core):
        ref = place(j, w, spot((a, a_dn, a_up, a_op)[i], near[r]), core)
        return send(ref, ref, d_s.at[j, 4 * i + r], d_r.at[j, 4 * i + r], partner)

    def have(j, w, r):
        g2(j, w, r, 1).start()
        g2(j, w, r, 0).start()
        d2d(j, w, 0, r, c).start()

    def u(j, w, wp):
        for k in (2, 3, 4, 5):
            b_msg(j, w, k).wait_recv()
        for half, dep, ind in ((0, 4, 3), (1, 5, 2)):
            r0, nr = ROWS[half]
            v = hf_v[j, b, r0:r0 + nr, 0:w] + rb_v[j, dep, 0:nr, 0:w].astype(F32)
            v += rb_v[j, ind, 0:nr, 0:w].astype(F32)
            v = base_v[c * 3 + j, r0:r0 + nr, 0:w] - scale * v
            out_ref[mine, r0:r0 + nr, cols(j, w, c)] = v.astype(BF16)
        g1(j, w, 0).start()
        g1(j, w, 1).start()
        have(j, w, 0)

    def a1(j, w, wp):
        g1(j, w, 0).wait_recv()
        g1(j, w, 2).start()
        g1(j, w, 1).wait_recv()
        g1(j, w, 3).start()
        have(j, w, 1)
        have(j, w, 2)

    def a2(j, w, wp):
        g1(j, w, 2).wait_recv()
        g1(j, w, 3).wait_recv()
        have(j, w, 3)

    def a3(j, w, wp):
        for r in range(4):
            g2(j, w, r, 1).wait_recv()
            if r < 2:
                g3(j, w, r).start()
            d2d(j, w, 1, r, c).start()
            g2(j, w, r, 0).wait_recv()
            if r >= 2:
                g3(j, w, r).start()
            d2d(j, w, 2, r, c).start()

    def a4(j, w, wp):
        for r in range(4):
            g3(j, w, r).wait_recv()
            d2d(j, w, 3, r, c).start()

    def last(j, w, wp):
        for i in range(4):
            for r in range(4):
                d2d(j, wp, i, r, 1 - c).wait_recv()
                d2d(j, w, i, r, c).wait_send()
        p_send(j, wp).wait_send()
        for k in range(6):
            a_msg(j, w, k).wait_send()
            b_msg(j, w, k).wait_send()
        for k in range(4):
            g1(j, w, k).wait_send()
            g3(j, w, k).wait_send()
            g2(j, w, k, 0).wait_send()
            g2(j, w, k, 1).wait_send()

    def run(fn, j):
        if j < 2:
            fn(j, WIDE, WIDE)
        else:
            @pl.when(c == 0)
            def _():
                fn(2, WIDE, LANES)

            @pl.when(c == 1)
            def _():
                fn(2, LANES, WIDE)

    order = [(part, 0), (part, 1), (own, 0), (part, 2), (own, 1), (r1, 0), (own, 2), (r1, 1), (r2, 0), (r1, 2),
             (r3, 0), (r2, 1), (u, 0), (r3, 1), (r2, 2), (a1, 0), (u, 1), (r3, 2), (a2, 0), (a1, 1), (u, 2),
             (a2, 1), (a1, 2), (a3, 0), (a2, 2), (a3, 1), (a4, 0), (a3, 2), (a4, 1), (a4, 2),
             (last, 0), (last, 1), (last, 2)]
    for fn, j in order:
        run(fn, j)
    nz.wait_send()

    def st_end(blk, _):
        for k in range(1, n_cls):
            st_copy(blk, k).wait_send()
        return 0

    lax.fori_loop(0, rows // 256, st_end, 0)


def local(features, labels, weight, noise):
    rows, depth = features.shape
    width = weight.shape[1]
    n_cls = lax.axis_size("cls")
    scale = 0.1 * (width * n_cls) / (rows * lax.axis_size("ex"))
    any_spec = pl.BlockSpec(memory_space=pl.ANY)
    vmem = pl.BlockSpec(memory_space=pltpu.VMEM)
    dma = pltpu.SemaphoreType.DMA
    blocks = rows // 256
    out = pl.pallas_call(
        functools.partial(kernel, scale),
        out_shape=jax.ShapeDtypeStruct((16, 104, width), BF16),
        in_specs=[any_spec, vmem, any_spec, any_spec],
        out_specs=vmem,
        scratch_shapes=[
            pltpu.VMEM((rows, depth), BF16),
            pltpu.VMEM((depth, width), BF16),
            pltpu.VMEM((depth, rows), BF16),
            pltpu.VMEM((rows, width), F32),
            pltpu.VMEM((6, rows, WIDE), BF16),
            pltpu.VMEM((rows, LANES), jnp.int32),
            pltpu.VMEM((LANES, LANES), F32),
            pltpu.VMEM((n_cls, blocks, 8, LANES), F32),
            pltpu.VMEM((blocks, 8, LANES), F32),
            pltpu.VMEM((3, depth, WIDE), F32),
            pltpu.VMEM((3, depth, WIDE), F32),
            pltpu.VMEM((3, 4, 4, 104, WIDE), BF16),
            pltpu.VMEM((3, 6, 2, 104, WIDE), BF16),
            pltpu.VMEM((3, 4, 104, WIDE), F32),
            pltpu.VMEM((3, 4, 104, WIDE), BF16),
            pltpu.VMEM((3, 6, 56, WIDE), BF16),
            pltpu.VMEM((6, 104, WIDE), F32),
            pltpu.VMEM((104, width), BF16),
            pltpu.VMEM((2, 52, width), BF16),
            dma((4,)), dma((blocks, n_cls - 1)), dma((blocks, n_cls - 1)), dma, dma,
            dma((3,)), dma((3,)), dma((3, 6)), dma((3, 6)), dma((3, 6)), dma((3, 6)),
            dma((3, 4)), dma((3, 4)), dma((3, 8)), dma((3, 8)), dma((3, 4)), dma((3, 4)),
            dma((3, 16)), dma((3, 16)),
        ],
        compiler_params=pltpu.CompilerParams(
            collective_id=0, has_side_effects=True, vmem_limit_bytes=67_043_328),
        cost_estimate=pl.CostEstimate(flops=4 * rows * depth * width, bytes_accessed=16_000_000, transcendentals=rows * width),
    )(features, labels.reshape(8, 128), weight, noise)
    return out.reshape(depth, width)


def solution(mesh):
    in_specs = (P("ex", None), P("ex"), P(None, "cls"), P("ex", "cls"))
    out_specs = P(None, "cls")
    return jax.shard_map(local, mesh=mesh, in_specs=in_specs, out_specs=out_specs, check_vma=False)
```

time: 257 us -> 83.7 us (0.33)
  blocking collectives: 88.6 us -> 0 us
  Pallas kernels: 0 us -> 78.7 us
  waiting for transfers between devices: 62.5 us -> 0 us
  starting transfers between devices: 30.5 us -> 0 us
  local copies, waits for them, and re-layouts: 28.4 us -> 4.85 us
  matrix products: 23.1 us -> 0 us
  between operations: 14.2 us -> 0.01 us
  other arithmetic: 8.44 us -> 0 us
    unnamed x1 -> x0, blocking collectives: 88.6 us -> none
    pallas_call x0 -> x1, Pallas kernels: none -> 78.7 us  [local(): pl.pallas_call(functools.partial(kernel, scale), out_shape=jax.ShapeDtype...]
    all_gather x1 -> x0, waiting for transfers between devices: 50.5 us -> none  [local(): lax.all_gather(updated.astype(jnp.bfloat16), 'ex', axis=1, tiled=True)]
    all_to_all x3 -> x0, starting transfers between devices: 25.5 us -> none  [the longest x2 15.8 us: copy_for_each(): return lax.all_to_all(copies, axis, split_axis=0, concat_axis=0, tiled=True)]
    dot_general x2 -> x0, matrix products: 23.1 us -> none  [the longest x1 12.5 us: local(): lax.dot_general(features, coef, (((0,), (0,)), ((), ())), preferred_eleme...]
    unnamed x20 -> x1, local copies, waits for them, and re-layouts: 19.9 us -> 4.85 us
    reduce_sum x3 -> x0, other arithmetic: 6.86 us -> none  [the longest x1 3.96 us: local(): jnp.sum(expo, axis=1)]
    all_to_all x3 -> x0, waiting for transfers between devices: 6.25 us -> none  [the longest x2 6.25 us: copy_for_each(): return lax.all_to_all(copies, axis, split_axis=0, concat_axis=0, tiled=True)]
  transfers between devices with their start and end apart: 7 -> 0, of which waited for: 3 -> 0; matrix products, arithmetic and copies ran while one was open for 44% -> 0% of each run, Pallas kernels for 0% -> 0%
where the time goes in v1:
time: 83.7 us; the launch traced here: 83.6 us
  Pallas kernels  78.7 us (94%)
  local copies, waits for them, and re-layouts  4.85 us (6%)
    pallas_call x1, Pallas kernels, local(): pl.pallas_call(functools.partial(kernel, scale), out_shape=jax.ShapeDtype...  78.7 us
    unnamed x1, local copies, waits for them, and re-layouts  4.85 us

profile of v1, /device:TPU:1, one launch (start us, length us, event | category | flops | bytes accessed | tf_op | source)
XLA Modules:
  0.0 83.6 jit_solution(2786202782630813503)
XLA Ops:
  0.0 78.7 %shard_map.46 = bf16[16,104,1408]{2,1,0:T(8,128)(2,1)} custom-call(bf16[1024,1664]{1,0:T(8,128)(2,1)} %f_hbm.1, s32[8,128]{1,0:T(8,128)} %bitcast.3, bf16[1664,1408]{1,0:T(8,128)(2,1)} %w_hbm.1, bf16[52,1408]{1,0:T(8,128)(2,1)} %noise_hbm.1), custom_call_target="tpu_custom_call" | custom-call | flops 9596567552 | bytes 16000000 | tf_op jit(solution)/shard_map/pallas_call | solution.py:371
  78.7 4.8 %copy.6 = bf16[1664,1408]{1,0:T(8,128)(2,1)} copy(bf16[1664,1408]{1,0:T(8,128)(2,1)} %bitcast.2) | data formatting | bytes 9371648

commit v2 on v0

v2 whole, which is shorter than its diff:
```python
import functools

import jax
import jax.numpy as jnp
from jax import lax
from jax.experimental import pallas as pl
from jax.experimental.pallas import tpu as pltpu
from jax.sharding import PartitionSpec as P

MESH = pl.DeviceIdType.MESH
F32, BF16 = jnp.float32, jnp.bfloat16
CLIP = 48.0
WIDE = 256
LANES = 128
ROWS = ((0, 48), (48, 56))

ORDER = " ".join((
    "part0 part1 own0 opp0", "ind0 opp1 own1 ind1", "opp3 part2 opp2 ind2",
    "r10 ind3 own2 opp4", "r11 r13 opp5 r12", "r20 ind4 r14 r21",
    "ind5 r23 r15 r30", "r22 r31 r24 r33", "u0 r32 r25 r34",
    "u1 u3 a10 u2", "r35 u4 a11 a12", "u5 a13 a21 a14",
    "a22 a15 a23 a20", "a31 a24 a25 a32", "a33 a30 a34 a35",
    "a43 a40 a41 a42", "a44 a45",
))


def kernel(scale, f_hbm, lab_hbm, w_hbm, noise_hbm, out_ref,
           f_v, w_v, ft_v, e_v, coef_v, lab_v, labrow_v, xt_v, st_v, fn_v, psend_v, precv_v,
           g_v, ra_v, hf_v, hs_v, rb_v, base_v, wown_v, nz_v,
           ld_sem, w_sem, f_sem, st_s, st_r, nz_s, nz_r, p_s, p_r, out_s, in_r):
    rows, depth = f_hbm.shape
    width = w_hbm.shape[1]
    tiles = width // LANES
    blocks = rows // WIDE
    n_cls = lax.axis_size("cls")
    ex = lax.axis_index("ex")
    z = lax.axis_index("cls")
    core = ex % 2
    c = 1 - core
    x = ex // 8
    y = (ex // 2) % 4
    a = x * (1 - c) + y * c
    b = y * (1 - c) + x * c

    def spot(i, j):
        return i * (4 - 3 * c) + j * (1 + 3 * c)

    def dev(i, j):
        return spot(i, j) * 2 + core

    mine = spot(a, b)
    a_up, a_dn, a_op = (a + 1) % 4, (a + 3) % 4, (a + 2) % 4
    b_up, b_dn, b_op = (b + 1) % 4, (b + 3) % 4, (b + 2) % 4
    to_aup, to_adn = dev(a_up, b), dev(a_dn, b)
    to_bup, to_bdn = dev(a, b_up), dev(a, b_dn)
    partner = ex + 1 - 2 * core

    w_tiles = [(n, min(WIDE, width - n)) for n in range(0, width, WIDE)]

    def f_load(i):
        r = pl.ds(i * WIDE, WIDE)
        return pltpu.make_async_copy(f_hbm.at[r, :], f_v.at[r, :], f_sem.at[i])

    w_load = pltpu.make_async_copy(w_hbm, w_v, w_sem)

    lab_load = pltpu.make_async_copy(lab_hbm, labrow_v, ld_sem.at[0])
    own_load = pltpu.make_async_copy(
        w_hbm.at[pl.ds(pl.multiple_of(mine * 104, 8), 104), :], wown_v, ld_sem.at[1])
    nz_load = pltpu.make_async_copy(noise_hbm, nz_v.at[core], ld_sem.at[2])
    lab_load.start()
    f_load(0).start()
    w_load.start()

    barrier = pltpu.get_barrier_semaphore()
    for t in (to_aup, to_adn, to_bup, to_bdn, partner):
        pl.semaphore_signal(barrier, inc=1, device_id={"ex": t}, device_id_type=MESH)
    for k in range(1, n_cls):
        pl.semaphore_signal(barrier, inc=1, device_id={"cls": (z + k) % n_cls}, device_id_type=MESH)

    def send(src, dst, s, r, t):
        return pltpu.make_async_remote_copy(
            src_ref=src, dst_ref=dst, send_sem=s, recv_sem=r, device_id={"ex": t}, device_id_type=MESH)

    coef_v[5, :, LANES:] = jnp.zeros((rows, LANES), BF16)
    lane = lax.broadcasted_iota(jnp.int32, (64, LANES), 1)

    def st_copy(blk, k):
        return pltpu.make_async_remote_copy(
            src_ref=st_v.at[z, blk], dst_ref=st_v.at[z, blk], send_sem=st_s, recv_sem=st_r.at[blk], device_id={"cls": (z + k) % n_cls}, device_id_type=MESH)

    def sums(blk, i):
        h, s = i // 2, i % 2
        r = slice(blk * WIDE + i * 64, blk * WIDE + (i + 1) * 64)
        top = e_v[r, 0:LANES]
        for n in range(1, tiles):
            top = jnp.maximum(top, e_v[r, n * LANES:(n + 1) * LANES])
        top = jnp.max(top, axis=1, keepdims=True)
        lab = lab_v[r, :]
        zero = jnp.zeros((64, LANES), F32)
        one, two, hit, sq = zero, zero, zero, zero
        for n in range(tiles):
            v = jnp.exp(e_v[r, n * LANES:(n + 1) * LANES] - top)
            e_v[r, n * LANES:(n + 1) * LANES] = v
            one += v
            two += v * v
            hit += jnp.where(lane + n * LANES == lab, v, 0.0)
        for k in range(depth // LANES):
            v = f_v[r, k * LANES:(k + 1) * LANES].astype(F32)
            sq += v * v
        one = jnp.sum(one, axis=1, keepdims=True)
        two = jnp.sum(two, axis=1, keepdims=True)
        hit = jnp.sum(hit, axis=1, keepdims=True)
        sq = jnp.sum(sq, axis=1, keepdims=True)
        pick = jnp.where(lane == 4 * h, top, 0.0)
        pick = jnp.where(lane == 4 * h + 1, one, pick)
        pick = jnp.where(lane == 4 * h + 2, two, pick)
        pick = jnp.where(lane == 4 * h + 3, hit, pick)
        pick = jnp.where(lane == 8 + h, sq, pick)
        if h == 0:
            xt_v[blk, s * 64:(s + 1) * 64, :] = pick
        else:
            xt_v[blk, s * 64:(s + 1) * 64, :] += pick

    def labels_of(blk):
        if blk == 0:
            lab_load.wait()
        for i in (2 * blk, 2 * blk + 1):
            row = jnp.broadcast_to(labrow_v[i:i + 1, :].astype(F32), (LANES, LANES))
            lab_v[i * LANES:(i + 1) * LANES, :] = row.T.astype(jnp.int32) - z * width

    def forward(blk):
        r = slice(blk * WIDE, (blk + 1) * WIDE)
        if blk < blocks:
            with jax.named_scope("load"):
                f_load(blk).wait()
            with jax.named_scope("labels"):
                labels_of(blk)
            if blk == 0:
                for i in range(1, blocks):
                    f_load(i).start()
                with jax.named_scope("wload"):
                    w_load.wait()
        for i, (n, w) in enumerate(w_tiles):
            if blk < blocks:
                e_v[r, n:n + w] = jnp.dot(f_v[r, :], w_v[:, n:n + w], preferred_element_type=F32)
            if blk > 0 and i < 4:
                sums(blk - 1, i)
        if blk == 0:
            own_load.start()
            nz_load.start()
        if blk == 1:
            pl.semaphore_wait(barrier, 5 + n_cls - 1)
        if blk > 0:
            t = xt_v[blk - 1].T
            st_v[z, blk - 1] = t[0:8]
            fn_v[blk - 1] = t[8:16]
            for k in range(1, n_cls):
                st_copy(blk - 1, k).start()

    for blk in range(blocks + 1):
        with jax.named_scope(f"forward_{blk}"):
            forward(blk)

    with jax.named_scope("turn"):
        nz = send(noise_hbm, nz_v.at[core], nz_s, nz_r, partner)
        nz.start()

        def turn(i, _):
            r = pl.ds(pl.multiple_of(i * LANES, LANES), LANES)
            ft_v[:, r] = f_v[r, :].T
            return 0

        lax.fori_loop(0, rows // LANES, turn, 0)

    def weigh(blk, _):
        ref = st_v.at[pl.ds(0, n_cls - 1), blk]
        send(ref, ref, st_s, st_r.at[blk], partner).wait_recv()
        for h in range(2):
            tops = [st_v[p, blk, 4 * h:4 * h + 1, :] for p in range(n_cls)]
            top = functools.reduce(jnp.maximum, tops)
            total = jnp.zeros((1, LANES), F32)
            squares, hit = total, total
            for p in range(n_cls):
                g = jnp.exp(tops[p] - top)
                total += st_v[p, blk, 4 * h + 1:4 * h + 2, :] * g
                squares += st_v[p, blk, 4 * h + 2:4 * h + 3, :] * (g * g)
                hit += st_v[p, blk, 4 * h + 3:4 * h + 4, :] * g
            prob = hit / total
            miss = 1.0 - prob
            resid = jnp.maximum(squares / (total * total) - prob * prob, 0.0) + miss * miss
            norm = jnp.sqrt(fn_v[blk, h:h + 1, :]) * jnp.sqrt(resid)
            factor = CLIP / jnp.maximum(norm, CLIP)
            up = factor * jnp.exp(st_v[z, blk, 4 * h:4 * h + 1, :] - top) / total
            up = jnp.broadcast_to(up, (LANES, LANES)).T
            down = jnp.broadcast_to(factor, (LANES, LANES)).T
            for s in range(2):
                r = pl.ds(pl.multiple_of(blk * WIDE + h * 128 + s * 64, 64), 64)
                lab = lab_v[r, :]
                u, d = up[s * 64:(s + 1) * 64], down[s * 64:(s + 1) * 64]
                for n in range(tiles):
                    v = e_v[r, n * LANES:(n + 1) * LANES] * u
                    v -= jnp.where(lane + n * LANES == lab, d, 0.0)
                    coef_v[n // 2, r, (n % 2) * LANES:(n % 2 + 1) * LANES] = v.astype(BF16)
        return 0

    with jax.named_scope("weigh012"):
        lax.fori_loop(0, blocks - 1, weigh, 0)
    with jax.named_scope("base"):
        own_load.wait()
        nz_load.wait()
        nz.wait_recv()
        for n in range(tiles):
            cols = slice(n * LANES, (n + 1) * LANES)
            base_v[n] = wown_v[:, cols].astype(F32)
            for i in range(2):
                base_v[n, i * 52:(i + 1) * 52] -= (scale * 0.96 * CLIP) * nz_v[i, :, cols].astype(F32)
    with jax.named_scope("weigh3"):
        weigh(blocks - 1, 0)

    half = depth // 2

    def p_send(k, i):
        r = pl.ds(pl.multiple_of(i * half, 16), half)
        return send(psend_v.at[k, r, :], precv_v.at[k, r, :], p_s, p_r.at[k, i], partner)

    def strip(i, m):
        return pl.ds(pl.multiple_of(i * half + m * 208, 16), 208)

    def part(k):
        def body(i, _):
            for m in range(4):
                psend_v[k, strip(i, m), :] = jnp.dot(
                    ft_v[strip(i, m), :], coef_v[(1 - c) * 3 + k], preferred_element_type=F32).astype(BF16)
            p_send(k, i).start()
            return 0
        lax.fori_loop(0, 2, body, 0)

    def own(k):
        def body(i, _):
            p_send(k, i).wait_recv()
            for m in range(4):
                acc = jnp.dot(ft_v[strip(i, m), :], coef_v[c * 3 + k], preferred_element_type=F32)
                acc += precv_v[k, strip(i, m), :].astype(F32)
                for n in range(2):
                    q = spot(2 * i + m // 2, 2 * (m % 2) + n)
                    for h in range(2):
                        g_v[2 * k + h, q // 4, q % 4] = acc[
                            n * 104:(n + 1) * 104, h * LANES:(h + 1) * LANES].astype(BF16)
            return 0
        lax.fori_loop(0, 2, body, 0)

    def arrived(ref, j, k):
        send(ref, ref, out_s.at[0], in_r.at[j, k], partner).wait_recv()

    def a_msg(j, k):
        group, hf, t = ((a_op, 0, to_aup), (a_op, 1, to_adn), (a_up, 1, to_aup),
                        (a_dn, 0, to_adn), (a_up, 0, to_aup), (a_dn, 1, to_adn))[k]
        return send(g_v.at[j, group, pl.ds(2 * hf, 2)], ra_v.at[j, k], out_s.at[0], in_r.at[j, 0 if k < 2 else 1], t)

    def b_msg(j, k):
        piece, hf, t = ((b_op, 0, to_bup), (b_op, 1, to_bdn), (b_up, 1, to_bup),
                        (b_dn, 0, to_bdn), (b_up, 0, to_bup), (b_dn, 1, to_bdn))[k]
        r0, nr = ROWS[hf]
        return send(hs_v.at[j, piece, pl.ds(r0, nr)], rb_v.at[j, k, pl.ds(0, nr)],
                    out_s.at[1], in_r.at[j, 2 if k < 2 else 3], t)

    def opp(j):
        a_msg(j, 0).start()
        a_msg(j, 1).start()

    def ind(j):
        a_msg(j, 2).start()
        a_msg(j, 3).start()

    def r1(j):
        arrived(ra_v.at[j, pl.ds(0, 2)], j, 0)
        for k, group, hf in ((0, a_up, 0), (1, a_dn, 1)):
            for i in range(2):
                v = g_v[j, group, 2 * hf + i].astype(F32) + ra_v[j, k, i].astype(F32)
                g_v[j, group, 2 * hf + i] = v.astype(BF16)
            a_msg(j, 4 + k).start()

    def r2(j):
        arrived(ra_v.at[j, pl.ds(2, 4)], j, 1)
        for hf, dep, alone in ((0, 4, 3), (1, 5, 2)):
            for i in range(2):
                v = g_v[j, a, 2 * hf + i].astype(F32) + ra_v[j, dep, i].astype(F32)
                v += ra_v[j, alone, i].astype(F32)
                hf_v[j, 2 * hf + i] = v
                hs_v[j, 2 * hf + i] = v.astype(BF16)
        for k in range(4):
            b_msg(j, k).start()

    def r3(j):
        arrived(hs_v.at[j, 0], j, 2)
        for k, piece, hf in ((0, b_up, 0), (1, b_dn, 1)):
            r0, nr = ROWS[hf]
            v = hf_v[j, piece, r0:r0 + nr] + rb_v[j, k, 0:nr].astype(F32)
            hs_v[j, piece, r0:r0 + nr] = v.astype(BF16)
            b_msg(j, 4 + k).start()

    def cols(j):
        return pl.ds(pl.multiple_of((c * 6 + j) * LANES, LANES), LANES)

    def place(j, p, hf=None):
        if hf is None:
            return out_ref.at[p, :, cols(j)]
        return out_ref.at[p, pl.ds(*ROWS[hf]), cols(j)]

    def g1(j, k):
        piece, hf, t = ((mine, None, to_bup), (mine, None, to_bdn),
                        (spot(a, b_dn), 0, to_bup), (spot(a, b_up), 1, to_bdn))[k]
        ref = place(j, piece, hf)
        return send(ref, ref, out_s.at[2], in_r.at[j, 4 if k < 2 else 5], t)

    near = (b, b_dn, b_up, b_op)

    def g2(j, r, up):
        ref = place(j, spot(a, near[r]))
        return send(ref, ref, out_s.at[3], in_r.at[j, 6 + r], to_aup if up else to_adn)

    def g3(j, r):
        ref = place(j, spot(a_dn if r < 2 else a_up, near[r]))
        return send(ref, ref, out_s.at[4], in_r.at[j, 10], to_aup if r < 2 else to_adn)

    def d2d(j, i, r):
        ref = place(j, spot((a, a_dn, a_up, a_op)[i], near[r]))
        return send(ref, ref, out_s.at[5], in_r.at[j, 11], partner)

    def have(j, r):
        g2(j, r, 1).start()
        g2(j, r, 0).start()
        d2d(j, 0, r).start()

    def u(j):
        arrived(hs_v.at[j, pl.ds(0, 2)], j, 3)
        for hf, dep, alone in ((0, 4, 3), (1, 5, 2)):
            r0, nr = ROWS[hf]
            v = hf_v[j, b, r0:r0 + nr] + rb_v[j, dep, 0:nr].astype(F32)
            v += rb_v[j, alone, 0:nr].astype(F32)
            v = base_v[c * 6 + j, r0:r0 + nr] - scale * v
            out_ref[mine, r0:r0 + nr, cols(j)] = v.astype(BF16)
        g1(j, 0).start()
        g1(j, 1).start()
        have(j, 0)

    def a1(j):
        arrived(hs_v.at[j, pl.ds(0, 2)], j, 4)
        g1(j, 2).start()
        g1(j, 3).start()
        have(j, 1)
        have(j, 2)

    def a2(j):
        arrived(hs_v.at[j, 0], j, 5)
        have(j, 3)

    def a3(j):
        for r in range(4):
            arrived(hs_v.at[j, pl.ds(0, 2)], j, 6 + r)
            g3(j, r).start()
            d2d(j, 1, r).start()
            d2d(j, 2, r).start()

    def a4(j):
        arrived(hs_v.at[j], j, 10)
        for r in range(4):
            d2d(j, 3, r).start()

    def run(fn, j, role=0):
        with jax.named_scope(f"{fn.__name__}_{j}"):
            if j < 5:
                fn(j)
            else:
                pl.when(c == role)(lambda: fn(j))

    stages = dict(part=part, own=own, opp=opp, ind=ind, r1=r1, r2=r2, r3=r3, u=u, a1=a1, a2=a2, a3=a3, a4=a4)
    for word in ORDER.split():
        name, j = word[:-1], int(word[-1])
        if name in ("part", "own"):
            with jax.named_scope(word):
                stages[name](j)
        else:
            run(stages[name], j)

    def drain(n):
        for k, ref in enumerate((ra_v.at[pl.ds(0, n)], hs_v.at[pl.ds(0, n), pl.ds(0, 3)], hs_v.at[pl.ds(0, n), pl.ds(0, 3)],
                                 g_v.at[pl.ds(0, n), pl.ds(0, 2)], hs_v.at[pl.ds(0, n)], g_v.at[pl.ds(0, n)])):
            send(ref, ref, out_s.at[k], in_r.at[0, 0], partner).wait_send()

    with jax.named_scope("partner"):
        for j in range(6):
            run(lambda k: arrived(g_v.at[k], k, 11), j, 1)
    with jax.named_scope("drain"):
        pl.when(c == 0)(lambda: drain(6))
        pl.when(c == 1)(lambda: drain(5))
    nz.wait_send()
    send(psend_v, precv_v, p_s, p_r.at[0, 0], partner).wait_send()
    ref = st_v.at[pl.ds(0, n_cls - 1)]
    send(ref, ref, st_s, st_r.at[0], partner).wait_send()


def local(features, labels, weight, noise):
    rows, depth = features.shape
    width = weight.shape[1]
    n_cls = lax.axis_size("cls")
    scale = 0.1 * (width * n_cls) / (rows * lax.axis_size("ex"))
    hbm = pl.BlockSpec(memory_space=pltpu.HBM)
    dma = pltpu.SemaphoreType.DMA
    blocks = rows // WIDE
    args = [pltpu.with_memory_space_constraint(v, pltpu.HBM)
            for v in (features, labels.reshape(rows // LANES, LANES), weight, noise)]
    out = pl.pallas_call(
        functools.partial(kernel, scale),
        out_shape=jax.ShapeDtypeStruct((16, 104, width), BF16),
        in_specs=[hbm] * 4,
        out_specs=pl.BlockSpec(memory_space=pltpu.VMEM),
        scratch_shapes=[
            pltpu.VMEM((rows, depth), BF16),
            pltpu.VMEM((depth, width), BF16),
            pltpu.VMEM((depth, rows), BF16),
            pltpu.VMEM((rows, width), F32),
            pltpu.VMEM((6, rows, WIDE), BF16),
            pltpu.VMEM((rows, LANES), jnp.int32),
            pltpu.VMEM((rows // LANES, LANES), jnp.int32),
            pltpu.VMEM((blocks, LANES, LANES), F32),
            pltpu.VMEM((n_cls, blocks, 8, LANES), F32),
            pltpu.VMEM((blocks, 8, LANES), F32),
            pltpu.VMEM((3, depth, WIDE), BF16),
            pltpu.VMEM((3, depth, WIDE), BF16),
            pltpu.VMEM((6, 4, 4, 104, LANES), BF16),
            pltpu.VMEM((6, 6, 2, 104, LANES), BF16),
            pltpu.VMEM((6, 4, 104, LANES), F32),
            pltpu.VMEM((6, 4, 104, LANES), BF16),
            pltpu.VMEM((6, 6, 56, LANES), BF16),
            pltpu.VMEM((width // LANES, 104, LANES), F32),
            pltpu.VMEM((104, width), BF16),
            pltpu.VMEM((2, 52, width), BF16),
            dma((3,)), dma, dma((blocks,)), dma, dma((blocks,)), dma, dma,
            dma, dma((3, 2)), dma((6,)), dma((6, 12)),
        ],
        compiler_params=pltpu.CompilerParams(
            collective_id=0, has_side_effects=True, vmem_limit_bytes=48_000_000),
        cost_estimate=pl.CostEstimate(flops=4 * rows * depth * width, bytes_accessed=16_000_000,
                                      transcendentals=rows * width),
    )(*args)
    return out.reshape(depth, width)


def solution(mesh):
    in_specs = (P("ex", None), P("ex"), P(None, "cls"), P("ex", "cls"))
    out_specs = P(None, "cls")
    return jax.shard_map(local, mesh=mesh, in_specs=in_specs, out_specs=out_specs, check_vma=False)
```

time: 257 us -> 66 us (0.26)
  blocking collectives: 88.6 us -> 0 us
  Pallas kernels: 0 us -> 63.8 us
  waiting for transfers between devices: 62.5 us -> 0 us
  starting transfers between devices: 30.5 us -> 0 us
  local copies, waits for them, and re-layouts: 28.4 us -> 2.18 us
  matrix products: 23.1 us -> 0 us
  between operations: 14.2 us -> 0.01 us
  other arithmetic: 8.44 us -> 0 us
    unnamed x1 -> x0, blocking collectives: 88.6 us -> none
    pallas_call x0 -> x1, Pallas kernels: none -> 63.8 us  [local(): pl.pallas_call(functools.partial(kernel, scale), out_shape=jax.ShapeDtype...]
    all_gather x1 -> x0, waiting for transfers between devices: 50.5 us -> none  [local(): lax.all_gather(updated.astype(jnp.bfloat16), 'ex', axis=1, tiled=True)]
    all_to_all x3 -> x0, starting transfers between devices: 25.5 us -> none  [the longest x2 15.8 us: copy_for_each(): return lax.all_to_all(copies, axis, split_axis=0, concat_axis=0, tiled=True)]
    dot_general x2 -> x0, matrix products: 23.1 us -> none  [the longest x1 12.5 us: local(): lax.dot_general(features, coef, (((0,), (0,)), ((), ())), preferred_eleme...]
    unnamed x20 -> x1, local copies, waits for them, and re-layouts: 19.9 us -> 2.18 us
    reduce_sum x3 -> x0, other arithmetic: 6.86 us -> none  [the longest x1 3.96 us: local(): jnp.sum(expo, axis=1)]
    all_to_all x3 -> x0, waiting for transfers between devices: 6.25 us -> none  [the longest x2 6.25 us: copy_for_each(): return lax.all_to_all(copies, axis, split_axis=0, concat_axis=0, tiled=True)]
  transfers between devices with their start and end apart: 7 -> 0, of which waited for: 3 -> 0; matrix products, arithmetic and copies ran while one was open for 44% -> 0% of each run, Pallas kernels for 0% -> 0%
where the time goes in v2:
time: 66 us
  Pallas kernels  63.8 us (97%)
  local copies, waits for them, and re-layouts  2.18 us (3%)
    pallas_call x1, Pallas kernels, local(): pl.pallas_call(functools.partial(kernel, scale), out_shape=jax.ShapeDtype...  63.8 us
    unnamed x1, local copies, waits for them, and re-layouts  2.18 us

profile of v2, /device:TPU:1, one launch (start us, length us, event | category | flops | bytes accessed | tf_op | source)
XLA Modules:
  0.0 66.0 jit_solution(9320162315770863538)
XLA Ops:
  0.0 63.8 %shard_map.46 = bf16[16,104,1408]{2,1,0:T(8,128)(2,1)S(1)} custom-call(bf16[1024,1664]{1,0:T(8,128)(2,1)} %f_hbm.1, s32[8,128]{1,0:T(8,128)} %bitcast.3, bf16[1664,1408]{1,0:T(8,128)(2,1)} %w_hbm.1, bf16[52,1408]{1,0:T(8,128)(2,1)} %noise_hbm.1), custom_call_target="tpu_custom_call" | custom-call | flops 9596567552 | bytes 16000000 | tf_op jit(solution)/shard_map/pallas_call | solution.py:413
  63.8 2.2 %copy.6 = bf16[1664,1408]{1,0:T(8,128)(2,1)} copy(bf16[1664,1408]{1,0:T(8,128)(2,1)S(1)} %bitcast.2) | data formatting | bytes 9371648

commit v3 on v2

--- a/solution.py
+++ b/solution.py
@@ -15,18 +15,22 @@
 ROWS = ((0, 48), (48, 56))
 
 ORDER = " ".join((
-    "part0 part1 own0 opp0", "ind0 opp1 own1 ind1", "opp3 part2 opp2 ind2",
-    "r10 ind3 own2 opp4", "r11 r13 opp5 r12", "r20 ind4 r14 r21",
-    "ind5 r23 r15 r30", "r22 r31 r24 r33", "u0 r32 r25 r34",
-    "u1 u3 a10 u2", "r35 u4 a11 a12", "u5 a13 a21 a14",
-    "a22 a15 a23 a20", "a31 a24 a25 a32", "a33 a30 a34 a35",
-    "a43 a40 a41 a42", "a44 a45",
+    "part0 part1 own0 opp1", "opp0 ind1 ind0 own1", "opp2 opp3 part2 ind3",
+    "r11 r10 ind2 own2", "opp4 r12 r13 r21", "opp5 r20 r30 ind4",
+    "r14 r22 r23 r31", "r15 ind5 u1 r33", "u0 r32 r24 u3",
+    "r25 r34 a11 a10", "u2 r35 u5 u4", "a13 a21 a23 a12",
+    "a22 a20 a15 a14", "a24 a25 a31 a33", "a32 a30 a34 a35",
+    "a40 a43 a41 a42", "a45 a44",
 ))
+FAR_RS_A = ()
+FAR_RS_B = (0, 1, 3, 4, 5)
+FAR_AG_B = (2, 3, 4, 5)
+FAR_AG_A = ()
 
 
 def kernel(scale, f_hbm, lab_hbm, w_hbm, noise_hbm, out_ref,
            f_v, w_v, ft_v, e_v, coef_v, lab_v, labrow_v, xt_v, st_v, fn_v, psend_v, precv_v,
-           g_v, ra_v, hf_v, hs_v, rb_v, base_v, wown_v, nz_v,
+           g_v, ra_v, hf_v, hs_v, rb_v, rf_v, base_v, wown_v, nz_v,
            ld_sem, w_sem, f_sem, st_s, st_r, nz_s, nz_r, p_s, p_r, out_s, in_r):
     rows, depth = f_hbm.shape
     width = w_hbm.shape[1]
@@ -53,6 +57,7 @@
     b_up, b_dn, b_op = (b + 1) % 4, (b + 3) % 4, (b + 2) % 4
     to_aup, to_adn = dev(a_up, b), dev(a_dn, b)
     to_bup, to_bdn = dev(a, b_up), dev(a, b_dn)
+    to_aop, to_bop = dev(a_op, b), dev(a, b_op)
     partner = ex + 1 - 2 * core
 
     w_tiles = [(n, min(WIDE, width - n)) for n in range(0, width, WIDE)]
@@ -61,7 +66,11 @@
         r = pl.ds(i * WIDE, WIDE)
         return pltpu.make_async_copy(f_hbm.at[r, :], f_v.at[r, :], f_sem.at[i])
 
-    w_load = pltpu.make_async_copy(w_hbm, w_v, w_sem)
+    parts = ((0, 768), (768, depth - 768))
+
+    def w_load(i):
+        r = pl.ds(*parts[i])
+        return pltpu.make_async_copy(w_hbm.at[r, :], w_v.at[r, :], w_sem.at[i])
 
     lab_load = pltpu.make_async_copy(lab_hbm, labrow_v, ld_sem.at[0])
     own_load = pltpu.make_async_copy(
@@ -69,10 +78,11 @@
     nz_load = pltpu.make_async_copy(noise_hbm, nz_v.at[core], ld_sem.at[2])
     lab_load.start()
     f_load(0).start()
-    w_load.start()
+    w_load(0).start()
+    w_load(1).start()
 
     barrier = pltpu.get_barrier_semaphore()
-    for t in (to_aup, to_adn, to_bup, to_bdn, partner):
+    for t in (to_aup, to_adn, to_aop, to_bup, to_bdn, to_bop, partner):
         pl.semaphore_signal(barrier, inc=1, device_id={"ex": t}, device_id_type=MESH)
     for k in range(1, n_cls):
         pl.semaphore_signal(barrier, inc=1, device_id={"cls": (z + k) % n_cls}, device_id_type=MESH)
@@ -128,6 +138,9 @@
             row = jnp.broadcast_to(labrow_v[i:i + 1, :].astype(F32), (LANES, LANES))
             lab_v[i * LANES:(i + 1) * LANES, :] = row.T.astype(jnp.int32) - z * width
 
+    def turn(i):
+        ft_v[:, i * LANES:(i + 1) * LANES] = f_v[i * LANES:(i + 1) * LANES, :].T
+
     def forward(blk):
         r = slice(blk * WIDE, (blk + 1) * WIDE)
         if blk < blocks:
@@ -135,21 +148,26 @@
                 f_load(blk).wait()
             with jax.named_scope("labels"):
                 labels_of(blk)
-            if blk == 0:
-                for i in range(1, blocks):
-                    f_load(i).start()
-                with jax.named_scope("wload"):
-                    w_load.wait()
+        if blk == 0:
+            for i in range(1, blocks):
+                f_load(i).start()
+            for i, (k, nk) in enumerate(parts):
+                w_load(i).wait()
+                for n, w in w_tiles:
+                    v = jnp.dot(f_v[r, k:k + nk], w_v[k:k + nk, n:n + w], preferred_element_type=F32)
+                    e_v[r, n:n + w] = v if i == 0 else v + e_v[r, n:n + w]
         for i, (n, w) in enumerate(w_tiles):
-            if blk < blocks:
+            if 0 < blk < blocks:
                 e_v[r, n:n + w] = jnp.dot(f_v[r, :], w_v[:, n:n + w], preferred_element_type=F32)
             if blk > 0 and i < 4:
                 sums(blk - 1, i)
+            if 0 < blk < blocks and i >= 4:
+                turn((blk - 1) * 2 + i - 4)
         if blk == 0:
             own_load.start()
             nz_load.start()
         if blk == 1:
-            pl.semaphore_wait(barrier, 5 + n_cls - 1)
+            pl.semaphore_wait(barrier, 7 + n_cls - 1)
         if blk > 0:
             t = xt_v[blk - 1].T
             st_v[z, blk - 1] = t[0:8]
@@ -165,12 +183,8 @@
         nz = send(noise_hbm, nz_v.at[core], nz_s, nz_r, partner)
         nz.start()
 
-        def turn(i, _):
-            r = pl.ds(pl.multiple_of(i * LANES, LANES), LANES)
-            ft_v[:, r] = f_v[r, :].T
-            return 0
-
-        lax.fori_loop(0, rows // LANES, turn, 0)
+        for i in (2 * blocks - 2, 2 * blocks - 1):
+            turn(i)
 
     def weigh(blk, _):
         ref = st_v.at[pl.ds(0, n_cls - 1), blk]
@@ -255,7 +269,15 @@
     def a_msg(j, k):
         group, hf, t = ((a_op, 0, to_aup), (a_op, 1, to_adn), (a_up, 1, to_aup),
                         (a_dn, 0, to_adn), (a_up, 0, to_aup), (a_dn, 1, to_adn))[k]
-        return send(g_v.at[j, group, pl.ds(2 * hf, 2)], ra_v.at[j, k], out_s.at[0], in_r.at[j, 0 if k < 2 else 1], t)
+        return send(g_v.at[j, group, pl.ds(2 * hf, 2)], ra_v.at[j, pl.ds(2 * k, 2)], out_s.at[0], in_r.at[j, 0 if k < 2 else 1], t)
+
+    def a_far(j, k):
+        group, t = ((a_op, to_aop), (a_up, to_aup), (a_dn, to_adn))[k]
+        return send(g_v.at[j, group], ra_v.at[j, pl.ds(4 * k, 4)], out_s.at[0], in_r.at[j, min(k, 1)], t)
+
+    def b_far(j, k):
+        piece, t = ((b_op, to_bop), (b_up, to_bup), (b_dn, to_bdn))[k]
+        return send(hs_v.at[j, piece], rf_v.at[j, k], out_s.at[1], in_r.at[j, 2 + min(k, 1)], t)
 
     def b_msg(j, k):
         piece, hf, t = ((b_op, 0, to_bup), (b_op, 1, to_bdn), (b_up, 1, to_bup),
@@ -265,33 +287,46 @@
                     out_s.at[1], in_r.at[j, 2 if k < 2 else 3], t)
 
     def opp(j):
+        if j in FAR_RS_A:
+            a_far(j, 0).start()
+            return
         a_msg(j, 0).start()
         a_msg(j, 1).start()
 
     def ind(j):
+        if j in FAR_RS_A:
+            a_far(j, 1).start()
+            a_far(j, 2).start()
+            return
         a_msg(j, 2).start()
         a_msg(j, 3).start()
 
     def r1(j):
-        arrived(ra_v.at[j, pl.ds(0, 2)], j, 0)
+        if j in FAR_RS_A:
+            return
+        arrived(ra_v.at[j, pl.ds(0, 4)], j, 0)
         for k, group, hf in ((0, a_up, 0), (1, a_dn, 1)):
             for i in range(2):
-                v = g_v[j, group, 2 * hf + i].astype(F32) + ra_v[j, k, i].astype(F32)
+                v = g_v[j, group, 2 * hf + i].astype(F32) + ra_v[j, 2 * k + i].astype(F32)
                 g_v[j, group, 2 * hf + i] = v.astype(BF16)
             a_msg(j, 4 + k).start()
 
     def r2(j):
-        arrived(ra_v.at[j, pl.ds(2, 4)], j, 1)
-        for hf, dep, alone in ((0, 4, 3), (1, 5, 2)):
-            for i in range(2):
-                v = g_v[j, a, 2 * hf + i].astype(F32) + ra_v[j, dep, i].astype(F32)
-                v += ra_v[j, alone, i].astype(F32)
-                hf_v[j, 2 * hf + i] = v
-                hs_v[j, 2 * hf + i] = v.astype(BF16)
-        for k in range(4):
-            b_msg(j, k).start()
+        if j in FAR_RS_A:
+            arrived(ra_v.at[j, pl.ds(0, 4)], j, 0)
+        arrived(ra_v.at[j, pl.ds(4, 8)], j, 1)
+        for i in range(4):
+            v = g_v[j, a, i].astype(F32)
+            for k in (i, 4 + i, 8 + i) if j in FAR_RS_A else ((8 + i, 6 + i) if i < 2 else (8 + i, 2 + i)):
+                v += ra_v[j, k].astype(F32)
+            hf_v[j, i] = v
+            hs_v[j, i] = v.astype(BF16)
+        for k in range(3 if j in FAR_RS_B else 4):
+            (b_far if j in FAR_RS_B else b_msg)(j, k).start()
 
     def r3(j):
+        if j in FAR_RS_B:
+            return
         arrived(hs_v.at[j, 0], j, 2)
         for k, piece, hf in ((0, b_up, 0), (1, b_dn, 1)):
             r0, nr = ROWS[hf]
@@ -330,24 +365,38 @@
     def have(j, r):
         g2(j, r, 1).start()
         g2(j, r, 0).start()
+        if j in FAR_AG_A:
+            ref = place(j, spot(a, near[r]))
+            send(ref, ref, out_s.at[4], in_r.at[j, 10], to_aop).start()
         d2d(j, 0, r).start()
 
     def u(j):
+        if j in FAR_RS_B:
+            arrived(hs_v.at[j, 0], j, 2)
         arrived(hs_v.at[j, pl.ds(0, 2)], j, 3)
         for hf, dep, alone in ((0, 4, 3), (1, 5, 2)):
             r0, nr = ROWS[hf]
-            v = hf_v[j, b, r0:r0 + nr] + rb_v[j, dep, 0:nr].astype(F32)
-            v += rb_v[j, alone, 0:nr].astype(F32)
+            v = hf_v[j, b, r0:r0 + nr]
+            if j in FAR_RS_B:
+                for k in range(3):
+                    v += rf_v[j, k, r0:r0 + nr].astype(F32)
+            else:
+                v += rb_v[j, dep, 0:nr].astype(F32)
+                v += rb_v[j, alone, 0:nr].astype(F32)
             v = base_v[c * 6 + j, r0:r0 + nr] - scale * v
             out_ref[mine, r0:r0 + nr, cols(j)] = v.astype(BF16)
         g1(j, 0).start()
         g1(j, 1).start()
+        if j in FAR_AG_B:
+            ref = place(j, mine)
+            send(ref, ref, out_s.at[2], in_r.at[j, 5], to_bop).start()
         have(j, 0)
 
     def a1(j):
         arrived(hs_v.at[j, pl.ds(0, 2)], j, 4)
-        g1(j, 2).start()
-        g1(j, 3).start()
+        if j not in FAR_AG_B:
+            g1(j, 2).start()
+            g1(j, 3).start()
         have(j, 1)
         have(j, 2)
 
@@ -358,7 +407,8 @@
     def a3(j):
         for r in range(4):
             arrived(hs_v.at[j, pl.ds(0, 2)], j, 6 + r)
-            g3(j, r).start()
+            if j not in FAR_AG_A:
+                g3(j, r).start()
             d2d(j, 1, r).start()
             d2d(j, 2, r).start()
 
@@ -429,14 +479,15 @@
             pltpu.VMEM((3, depth, WIDE), BF16),
             pltpu.VMEM((3, depth, WIDE), BF16),
             pltpu.VMEM((6, 4, 4, 104, LANES), BF16),
-            pltpu.VMEM((6, 6, 2, 104, LANES), BF16),
+            pltpu.VMEM((6, 12, 104, LANES), BF16),
             pltpu.VMEM((6, 4, 104, LANES), F32),
             pltpu.VMEM((6, 4, 104, LANES), BF16),
             pltpu.VMEM((6, 6, 56, LANES), BF16),
+            pltpu.VMEM((6, 3, 104, LANES), BF16),
             pltpu.VMEM((width // LANES, 104, LANES), F32),
             pltpu.VMEM((104, width), BF16),
             pltpu.VMEM((2, 52, width), BF16),
-            dma((3,)), dma, dma((blocks,)), dma, dma((blocks,)), dma, dma,
+            dma((3,)), dma((2,)), dma((blocks,)), dma, dma((blocks,)), dma, dma,
             dma, dma((3, 2)), dma((6,)), dma((6, 12)),
         ],
         compiler_params=pltpu.CompilerParams(

time: 66 us -> 61.7 us (0.935)
  Pallas kernels: 63.8 us -> 59.4 us
    pallas_call x1, Pallas kernels: 63.8 us -> 59.4 us  [local(): pl.pallas_call(functools.partial(kernel, scale), out_shape=jax.ShapeDtype...]
where the time goes in v3:
time: 61.7 us; the launch traced here: 61.6 us
  Pallas kernels  59.4 us (96%)
  local copies, waits for them, and re-layouts  2.18 us (4%)
    pallas_call x1, Pallas kernels, local(): pl.pallas_call(functools.partial(kernel, scale), out_shape=jax.ShapeDtype...  59.4 us
    unnamed x1, local copies, waits for them, and re-layouts  2.18 us

profile of v3, /device:TPU:1, one launch (start us, length us, event | category | flops | bytes accessed | tf_op | source)
XLA Modules:
  0.0 61.6 jit_solution(730536410109289857)
XLA Ops:
  0.0 59.4 %shard_map.46 = bf16[16,104,1408]{2,1,0:T(8,128)(2,1)S(1)} custom-call(bf16[1024,1664]{1,0:T(8,128)(2,1)} %f_hbm.1, s32[8,128]{1,0:T(8,128)} %bitcast.3, bf16[1664,1408]{1,0:T(8,128)(2,1)} %w_hbm.1, bf16[52,1408]{1,0:T(8,128)(2,1)} %noise_hbm.1), custom_call_target="tpu_custom_call" | custom-call | flops 9596567552 | bytes 16000000 | tf_op jit(solution)/shard_map/pallas_call | solution.py:463
  59.5 2.2 %copy.6 = bf16[1664,1408]{1,0:T(8,128)(2,1)} copy(bf16[1664,1408]{1,0:T(8,128)(2,1)S(1)} %bitcast.2) | data formatting | bytes 9371648

commit v4 on v3

--- a/solution.py
+++ b/solution.py
@@ -29,7 +29,7 @@
 
 
 def kernel(scale, f_hbm, lab_hbm, w_hbm, noise_hbm, out_ref,
-           f_v, w_v, ft_v, e_v, coef_v, lab_v, labrow_v, xt_v, st_v, fn_v, psend_v, precv_v,
+           f_v, w_v, ft_v, e_v, coef_v, lab_v, labrow_v, xt_v, st_v, fn_v, psend_v, precv_v, acc_v,
            g_v, ra_v, hf_v, hs_v, rb_v, rf_v, base_v, wown_v, nz_v,
            ld_sem, w_sem, f_sem, st_s, st_r, nz_s, nz_r, p_s, p_r, out_s, in_r):
     rows, depth = f_hbm.shape
@@ -107,25 +107,30 @@
         top = jnp.max(top, axis=1, keepdims=True)
         lab = lab_v[r, :]
         zero = jnp.zeros((64, LANES), F32)
-        one, two, hit, sq = zero, zero, zero, zero
+        one, two, hit = zero, zero, zero
         for n in range(tiles):
             v = jnp.exp(e_v[r, n * LANES:(n + 1) * LANES] - top)
             e_v[r, n * LANES:(n + 1) * LANES] = v
             one += v
             two += v * v
             hit += jnp.where(lane + n * LANES == lab, v, 0.0)
-        for k in range(depth // LANES):
-            v = f_v[r, k * LANES:(k + 1) * LANES].astype(F32)
-            sq += v * v
         one = jnp.sum(one, axis=1, keepdims=True)
         two = jnp.sum(two, axis=1, keepdims=True)
         hit = jnp.sum(hit, axis=1, keepdims=True)
-        sq = jnp.sum(sq, axis=1, keepdims=True)
         pick = jnp.where(lane == 4 * h, top, 0.0)
         pick = jnp.where(lane == 4 * h + 1, one, pick)
         pick = jnp.where(lane == 4 * h + 2, two, pick)
         pick = jnp.where(lane == 4 * h + 3, hit, pick)
-        pick = jnp.where(lane == 8 + h, sq, pick)
+        xt_v[blk, s * 64:(s + 1) * 64, :] += pick
+
+    def squares_of(blk, i):
+        h, s = i // 2, i % 2
+        r = slice(blk * WIDE + i * 64, blk * WIDE + (i + 1) * 64)
+        sq = jnp.zeros((64, LANES), F32)
+        for k in range(depth // LANES):
+            v = f_v[r, k * LANES:(k + 1) * LANES].astype(F32)
+            sq += v * v
+        pick = jnp.where(lane == 8 + h, jnp.sum(sq, axis=1, keepdims=True), 0.0)
         if h == 0:
             xt_v[blk, s * 64:(s + 1) * 64, :] = pick
         else:
@@ -161,6 +166,8 @@
                 e_v[r, n:n + w] = jnp.dot(f_v[r, :], w_v[:, n:n + w], preferred_element_type=F32)
             if blk > 0 and i < 4:
                 sums(blk - 1, i)
+            if blk < blocks and i < 4:
+                squares_of(blk, i)
             if 0 < blk < blocks and i >= 4:
                 turn((blk - 1) * 2 + i - 4)
         if blk == 0:
@@ -217,8 +224,55 @@
                     coef_v[n // 2, r, (n % 2) * LANES:(n % 2 + 1) * LANES] = v.astype(BF16)
         return 0
 
+    half = depth // 2
+
+    def p_send(k, i):
+        r = pl.ds(pl.multiple_of(i * half, 16), half)
+        return send(psend_v.at[k, r, :], precv_v.at[k, r, :], p_s, p_r.at[k, i], partner)
+
+    def strip(i, m):
+        return pl.ds(pl.multiple_of(i * half + m * 416, 16), 416)
+
+    early = rows // 2
+
+    def begin():
+        def body(i, _):
+            for m in range(2):
+                acc_v[strip(i, m), :] = jnp.dot(
+                    ft_v[strip(i, m), 0:early], coef_v[(1 - c) * 3, 0:early, :], preferred_element_type=F32)
+            return 0
+        lax.fori_loop(0, 2, body, 0)
+
+    def part(k):
+        def body(i, _):
+            for m in range(2):
+                r0 = early if k == 0 else 0
+                v = jnp.dot(ft_v[strip(i, m), r0:rows], coef_v[(1 - c) * 3 + k, r0:rows, :], preferred_element_type=F32)
+                psend_v[k, strip(i, m), :] = (v + acc_v[strip(i, m), :] if k == 0 else v).astype(BF16)
+            p_send(k, i).start()
+            return 0
+        lax.fori_loop(0, 2, body, 0)
+
+    def own(k):
+        def body(i, _):
+            p_send(k, i).wait_recv()
+            for m in range(2):
+                acc = jnp.dot(ft_v[strip(i, m), :], coef_v[c * 3 + k], preferred_element_type=F32)
+                acc += precv_v[k, strip(i, m), :].astype(F32)
+                for n in range(4):
+                    q = spot(2 * i + m, n)
+                    for h in range(2):
+                        g_v[2 * k + h, q // 4, q % 4] = acc[
+                            n * 104:(n + 1) * 104, h * LANES:(h + 1) * LANES].astype(BF16)
+            return 0
+        lax.fori_loop(0, 2, body, 0)
+
     with jax.named_scope("weigh012"):
-        lax.fori_loop(0, blocks - 1, weigh, 0)
+        lax.fori_loop(0, 2, weigh, 0)
+    with jax.named_scope("begin"):
+        begin()
+    with jax.named_scope("weigh2"):
+        weigh(2, 0)
     with jax.named_scope("base"):
         own_load.wait()
         nz_load.wait()
@@ -230,38 +284,6 @@
                 base_v[n, i * 52:(i + 1) * 52] -= (scale * 0.96 * CLIP) * nz_v[i, :, cols].astype(F32)
     with jax.named_scope("weigh3"):
         weigh(blocks - 1, 0)
-
-    half = depth // 2
-
-    def p_send(k, i):
-        r = pl.ds(pl.multiple_of(i * half, 16), half)
-        return send(psend_v.at[k, r, :], precv_v.at[k, r, :], p_s, p_r.at[k, i], partner)
-
-    def strip(i, m):
-        return pl.ds(pl.multiple_of(i * half + m * 208, 16), 208)
-
-    def part(k):
-        def body(i, _):
-            for m in range(4):
-                psend_v[k, strip(i, m), :] = jnp.dot(
-                    ft_v[strip(i, m), :], coef_v[(1 - c) * 3 + k], preferred_element_type=F32).astype(BF16)
-            p_send(k, i).start()
-            return 0
-        lax.fori_loop(0, 2, body, 0)
-
-    def own(k):
-        def body(i, _):
-            p_send(k, i).wait_recv()
-            for m in range(4):
-                acc = jnp.dot(ft_v[strip(i, m), :], coef_v[c * 3 + k], preferred_element_type=F32)
-                acc += precv_v[k, strip(i, m), :].astype(F32)
-                for n in range(2):
-                    q = spot(2 * i + m // 2, 2 * (m % 2) + n)
-                    for h in range(2):
-                        g_v[2 * k + h, q // 4, q % 4] = acc[
-                            n * 104:(n + 1) * 104, h * LANES:(h + 1) * LANES].astype(BF16)
-            return 0
-        lax.fori_loop(0, 2, body, 0)
 
     def arrived(ref, j, k):
         send(ref, ref, out_s.at[0], in_r.at[j, k], partner).wait_recv()
@@ -355,8 +377,8 @@
         return send(ref, ref, out_s.at[3], in_r.at[j, 6 + r], to_aup if up else to_adn)
 
     def g3(j, r):
-        ref = place(j, spot(a_dn if r < 2 else a_up, near[r]))
-        return send(ref, ref, out_s.at[4], in_r.at[j, 10], to_aup if r < 2 else to_adn)
+        ref = place(j, spot(a_dn if r < 1 else a_up, near[r]))
+        return send(ref, ref, out_s.at[4], in_r.at[j, 10], to_aup if r < 1 else to_adn)
 
     def d2d(j, i, r):
         ref = place(j, spot((a, a_dn, a_up, a_op)[i], near[r]))
@@ -478,6 +500,7 @@
             pltpu.VMEM((blocks, 8, LANES), F32),
             pltpu.VMEM((3, depth, WIDE), BF16),
             pltpu.VMEM((3, depth, WIDE), BF16),
+            pltpu.VMEM((depth, WIDE), F32),
             pltpu.VMEM((6, 4, 4, 104, LANES), BF16),
             pltpu.VMEM((6, 12, 104, LANES), BF16),
             pltpu.VMEM((6, 4, 104, LANES), F32),

time: 61.7 us -> 61.1 us (level)
  no operation moved by 1% of the time
where the time goes in v4:
time: 61.1 us
  Pallas kernels  58.9 us (96%)
  local copies, waits for them, and re-layouts  2.18 us (4%)
    pallas_call x1, Pallas kernels, local(): pl.pallas_call(functools.partial(kernel, scale), out_shape=jax.ShapeDtype...  58.9 us
    unnamed x1, local copies, waits for them, and re-layouts  2.18 us

profile of v4, /device:TPU:1, one launch (start us, length us, event | category | flops | bytes accessed | tf_op | source)
XLA Modules:
  0.0 61.1 jit_solution(16829867041574795050)
XLA Ops:
  0.0 58.9 %shard_map.46 = bf16[16,104,1408]{2,1,0:T(8,128)(2,1)S(1)} custom-call(bf16[1024,1664]{1,0:T(8,128)(2,1)} %f_hbm.1, s32[8,128]{1,0:T(8,128)} %bitcast.3, bf16[1664,1408]{1,0:T(8,128)(2,1)} %w_hbm.1, bf16[52,1408]{1,0:T(8,128)(2,1)} %noise_hbm.1), custom_call_target="tpu_custom_call" | custom-call | flops 9596567552 | bytes 16000000 | tf_op jit(solution)/shard_map/pallas_call | solution.py:485
  58.9 2.2 %copy.6 = bf16[1664,1408]{1,0:T(8,128)(2,1)} copy(bf16[1664,1408]{1,0:T(8,128)(2,1)S(1)} %bitcast.2) | data formatting | bytes 9371648

commit v5 on v4

--- a/solution.py
+++ b/solution.py
@@ -15,17 +15,17 @@
 ROWS = ((0, 48), (48, 56))
 
 ORDER = " ".join((
-    "part0 part1 own0 opp1", "opp0 ind1 ind0 own1", "opp2 opp3 part2 ind3",
-    "r11 r10 ind2 own2", "opp4 r12 r13 r21", "opp5 r20 r30 ind4",
-    "r14 r22 r23 r31", "r15 ind5 u1 r33", "u0 r32 r24 u3",
-    "r25 r34 a11 a10", "u2 r35 u5 u4", "a13 a21 a23 a12",
-    "a22 a20 a15 a14", "a24 a25 a31 a33", "a32 a30 a34 a35",
-    "a40 a43 a41 a42", "a45 a44",
+    "part0 part1 own0 opp1", "opp0 ind0 own1 ind1", "opp3 opp2 part2 ind2",
+    "ind3 r11 r10 own2", "opp5 opp4 r13 r12", "r21 r31 ind4 r15",
+    "r14 r23 ind5 r20", "r22 r33 r30 u1", "r24 r25 u3 r35",
+    "u0 a11 r32 u5", "u2 a13 r34 a21", "u4 a15 a12 a22",
+    "a10 a20 a23 a31", "a25 a14 a24 a32", "a30 a35 a33 a42",
+    "a34 a41 a40 a44", "a45 a43",
 ))
 FAR_RS_A = ()
-FAR_RS_B = (0, 1, 3, 4, 5)
-FAR_AG_B = (2, 3, 4, 5)
-FAR_AG_A = ()
+FAR_RS_B = (0, 1, 2, 3, 4, 5)
+FAR_AG_B = (0, 2, 4)
+FAR_AG_A = (4,)
 
 
 def kernel(scale, f_hbm, lab_hbm, w_hbm, noise_hbm, out_ref,

time: 61.1 us -> 60.9 us (level)
  no operation moved by 1% of the time
where the time goes in v5:
time: 60.9 us; the launch traced here: 60.8 us
  Pallas kernels  58.6 us (96%)
  local copies, waits for them, and re-layouts  2.18 us (4%)
    pallas_call x1, Pallas kernels, local(): pl.pallas_call(functools.partial(kernel, scale), out_shape=jax.ShapeDtype...  58.6 us
    unnamed x1, local copies, waits for them, and re-layouts  2.18 us

profile of v5, /device:TPU:1, one launch (start us, length us, event | category | flops | bytes accessed | tf_op | source)
XLA Modules:
  0.0 60.8 jit_solution(3943886222799220389)
XLA Ops:
  0.0 58.6 %shard_map.46 = bf16[16,104,1408]{2,1,0:T(8,128)(2,1)S(1)} custom-call(bf16[1024,1664]{1,0:T(8,128)(2,1)} %f_hbm.1, s32[8,128]{1,0:T(8,128)} %bitcast.3, bf16[1664,1408]{1,0:T(8,128)(2,1)} %w_hbm.1, bf16[52,1408]{1,0:T(8,128)(2,1)} %noise_hbm.1), custom_call_target="tpu_custom_call" | custom-call | flops 9596567552 | bytes 16000000 | tf_op jit(solution)/shard_map/pallas_call | solution.py:485
  58.6 2.2 %copy.6 = bf16[1664,1408]{1,0:T(8,128)(2,1)} copy(bf16[1664,1408]{1,0:T(8,128)(2,1)S(1)} %bitcast.2) | data formatting | bytes 9371648
